TPU v7x, 32 devices: a whole 2x2x4 slice. The times are simulated.
32 devices in a mesh: pop: 4 (over x, core), tp: 4 (over z), pp: 2 (over y).
Axes of the slice: x: 2, y: 2, z: 4, core: 2. Of those that a mesh axis runs over, the one named last changes fastest.
Arguments:
- hidden_in: bfloat16 [256, 8, 4096], P('tp', 'pop'), may hold values from -6 to 6
- norm_gain: float32 [2, 4096], P('pp'), may hold values from 0.5 to 1.5
- w_gate: bfloat16 [2, 4096, 12288], P('pp', None, 'tp'), may hold values from -0.09375 to 0.09375
- w_up: bfloat16 [2, 4096, 12288], P('pp', None, 'tp'), may hold values from -0.09375 to 0.09375
- w_down: bfloat16 [2, 12288, 4096], P('pp', 'tp'), may hold values from -0.0546875 to 0.0546875
- gate_left: bfloat16 [2, 8, 4096], P('pp', 'pop'), may hold values from -6 to 6
- gate_right: bfloat16 [2, 8, 12288], P('pp', 'pop', 'tp'), may hold values from -6 to 6
- up_left: bfloat16 [2, 8, 4096], P('pp', 'pop'), may hold values from -6 to 6
- up_right: bfloat16 [2, 8, 12288], P('pp', 'pop', 'tp'), may hold values from -6 to 6
- down_left: bfloat16 [2, 8, 12288], P('pp', 'pop', 'tp'), may hold values from -6 to 6
- down_right: bfloat16 [2, 8, 4096], P('pp', 'pop'), may hold values from -6 to 6
- ranks: int32 [8], P('pop'), may hold values from 0 to 7, each once
Outputs:
- section_out: bfloat16 [2, 256, 8, 4096], P('pp', 'tp', 'pop')
- update_gate: bfloat16 [2, 4096, 12288], P('pp', 'pop', 'tp')
- update_up: bfloat16 [2, 4096, 12288], P('pp', 'pop', 'tp')
- update_down: bfloat16 [2, 12288, 4096], P('pp', 'tp', 'pop')
Inputs may be any that keep to these rules, and one draw needn't show every extreme that they name: `ranks`: each number from 0 to 7 is the rank of exactly one member.
All inputs are finite; a program needn't handle non-finite values.
Results may differ from a plain program's by a relative error of at most 0.014.
Values may be sent and summed in bfloat16 or wider, within the bound.
A program may use at most 256 MiB of HBM per device.

v0:
```python
import math

import jax
import jax.numpy as jnp
from jax import lax
from jax.sharding import PartitionSpec as P

sigma_scale = 0.3
norm_eps = 1e-05


def normalized(block, gain):
    values = block.astype(jnp.float32)
    mean_sq = jnp.mean(values * values, axis=-1, keepdims=True)
    return (values * lax.rsqrt(mean_sq + norm_eps) * gain).astype(jnp.bfloat16)


def feed_forward(piece, w_gate, w_up, w_down, lefts, gate_right, up_right, down_left, down_right):
    coef_in = sigma_scale / math.sqrt(piece.shape[-1])
    coef_hidden = sigma_scale / math.sqrt(w_gate.shape[-1] * lax.axis_size("tp"))
    sides = coef_in * jnp.einsum("rd,vd->vr", piece, lefts, preferred_element_type=jnp.float32)
    gate = jnp.dot(piece, w_gate, preferred_element_type=jnp.float32)
    gate = gate + sides[0][:, None] * gate_right.astype(jnp.float32)[None]
    upper = jnp.dot(piece, w_up, preferred_element_type=jnp.float32)
    upper = upper + sides[1][:, None] * up_right.astype(jnp.float32)[None]
    inner = (jax.nn.silu(gate) * upper).astype(jnp.bfloat16)
    term = jnp.dot(inner, w_down, preferred_element_type=jnp.float32)
    down_side = coef_hidden * jnp.dot(inner, down_left, preferred_element_type=jnp.float32)
    return (term + down_side[:, None] * down_right.astype(jnp.float32)[None]).astype(jnp.bfloat16)


def grouped_outer(fitness, left, right, groups):
    weighted = fitness[:, None] * left.astype(jnp.float32)
    other = right.astype(jnp.float32)
    size = left.shape[0] // groups
    total = None
    for group in range(groups):
        part = None
        for member in range(group * size, (group + 1) * size):
            outer = weighted[member][:, None] * other[member][None, :]
            part = outer if part is None else part + outer
        part = lax.reduce_precision(part, 8, 7)
        total = part if total is None else total + part
    return total.astype(jnp.bfloat16)


def low_rank_updates(vectors, ranks):
    pop_size = lax.axis_size("pop")
    population = ranks.shape[0] * pop_size
    widths = [vector.shape[1] for vector in vectors]
    column = jnp.broadcast_to(ranks.astype(jnp.bfloat16)[:, None], (ranks.shape[0], 128))
    packed = jnp.concatenate(vectors + [column], axis=1)
    everyone = lax.all_gather(packed, "pop", axis=0, tiled=True)
    offsets = [sum(widths[:i]) for i in range(len(widths) + 1)]
    all_ranks = everyone[:, offsets[-1]]
    fitness = (2.0 * all_ranks.astype(jnp.float32) / (population - 1) - 1.0) / math.sqrt(population)
    gl, gr, ul, ur, dl, dr = [everyone[:, offsets[i] : offsets[i + 1]] for i in range(len(widths))]
    row_share = widths[0] // pop_size
    row_start = lax.axis_index("pop") * row_share

    def share(full):
        return lax.dynamic_slice_in_dim(full, row_start, row_share, 1)

    return (
        grouped_outer(fitness, share(gl), gr, pop_size),
        grouped_outer(fitness, share(ul), ur, pop_size),
        grouped_outer(fitness, dl, share(dr), pop_size),
    )


def per_device(
    hidden_in,
    norm_gain,
    w_gate,
    w_up,
    w_down,
    gate_left,
    gate_right,
    up_left,
    up_right,
    down_left,
    down_right,
    ranks,
):
    members = hidden_in.shape[1]
    sections = lax.axis_size("pp")
    section_index = lax.axis_index("pp")
    gain = norm_gain[0]
    vectors = [gate_left[0], gate_right[0], up_left[0], up_right[0], down_left[0], down_right[0]]
    updates = low_rank_updates(vectors, ranks)
    blocks = [hidden_in[:, k, :] for k in range(members)]
    outputs = blocks
    for section in range(sections):
        normed = [normalized(block, gain) for block in blocks]
        if section > 0:
            normed[0], terms[-1] = lax.optimization_barrier((normed[0], terms[-1]))
        pieces = [lax.all_gather(rows, "tp", axis=0, tiled=True) for rows in normed]
        terms = []
        for k in range(members):
            term = feed_forward(
                pieces[k],
                w_gate[0],
                w_up[0],
                w_down[0],
                jnp.stack([gate_left[0, k], up_left[0, k]]),
                gate_right[0, k],
                up_right[0, k],
                down_left[0, k],
                down_right[0, k],
            )
            if k + 1 < members:
                term, pieces[k + 1] = lax.optimization_barrier((term, pieces[k + 1]))
            terms.append(term)
        results = []
        for k in range(members):
            summed = lax.psum_scatter(terms[k], "tp", scatter_dimension=0, tiled=True)
            results.append((blocks[k].astype(jnp.float32) + summed.astype(jnp.float32)).astype(jnp.bfloat16))
        if section == 0:
            outputs = results
        else:
            outputs = [jnp.where(section_index == section, r, o) for r, o in zip(results, outputs)]
        if section + 1 < sections:
            blocks = [lax.ppermute(r, "pp", [(section, section + 1)]) for r in results]
            if section == 0:
                last, updates = lax.optimization_barrier((blocks[-1], updates))
                blocks = blocks[:-1] + [last]
    output = jnp.stack(outputs, axis=1)
    return (output[None], updates[0][None], updates[1][None], updates[2][None])


def solution(mesh):
    placed = (
        P("tp", "pop", None),
        P("pp", None),
        P("pp", None, "tp"),
        P("pp", None, "tp"),
        P("pp", "tp", None),
        P("pp", "pop", None),
        P("pp", "pop", "tp"),
        P("pp", "pop", None),
        P("pp", "pop", "tp"),
        P("pp", "pop", "tp"),
        P("pp", "pop", None),
        P("pop"),
    )
    return jax.shard_map(
        per_device,
        mesh=mesh,
        in_specs=placed,
        out_specs=(
            P("pp", "tp", "pop", None),
            P("pp", "pop", "tp"),
            P("pp", "pop", "tp"),
            P("pp", "tp", "pop"),
        ),
        check_vma=False,
    )
```

profile of v0, /device:TPU:6, one launch (start us, length us, event | category | flops | bytes accessed | tf_op | source)
XLA Modules:
  0.0 446.7 jit_solution(18126977525907759624)
XLA Ops:
  7.2 0.0 all-gather.6.cloned.1.call-start
  7.2 4.1 fusion.128
  11.4 1.2 fusion.104
  12.6 2.4 fusion.110
  15.0 0.0 all-gather.8.cloned.1.call-start
  15.1 0.7 all-gather.8.cloned.1.call-update
  15.8 0.0 reduce-scatter.7.cloned.1.call-start
  15.9 0.1 slice_bitcast_fusion
  16.2 0.1 constant_dynamic-update-slice_fusion
  16.3 6.2 %all-gather = bf16[4,2,21632]{2,1,0:T(2,128)(2,1)S(1)} all-gather(bf16[1,2,21632]{2,1,0:T(2,128)(2,1)S(1)} %bitcast.224), channel_id=1, replica_groups=mesh['pop'=4,'tp'=4,'pp'=2] {'pop'}, dimensions={0}, use_global_device_ids=true | all-gather | bytes 432640 | tf_op jit(solution)/shard_map/all_gather | solution.py:53
  22.5 0.1 reshape.132
  22.6 39.4 %all-gather.6.cloned.1.call-done = bf16[256,4096]{1,0:T(8,128)(2,1)} async-done(((bf16[64,4096]{1,0:T(8,128)(2,1)}), bf16[256,4096]{1,0:T(8,128)(2,1)}) %all-gather.6.cloned.1.call-update) | async-done | bytes 2097168 | tf_op jit(solution)/shard_map/all_gather | solution.py:97
  62.0 2.2 convolution_multiply_fusion.3
  64.3 12.9 %fusion.48 = f32[256,3072]{1,0:T(8,128)S(1)} fusion(bf16[256,4096]{1,0:T(8,128)(2,1)} %all-gather.6.cloned.1.call-done, bf16[1,4096,3072]{2,1,0:T(8,128)(2,1)} %param.14, f32[3072]{0:T(1024)S(1)} %bitcast.283, f32[256]{0:T(256)S(1)} %bitcast.300), kind=kOutput, calls=%fused_computation.35 | convolution fusion | flops 6444023808 | bytes 30422016 | tf_op jit(solution)/shard_map/dot_general | solution.py:22
  77.2 11.8 %fusion.93 = bf16[256,3072]{1,0:T(8,128)(2,1)S(1)} fusion(bf16[256,4096]{1,0:T(8,128)(2,1)S(1)} %copy-done.1, bf16[1,4096,3072]{2,1,0:T(8,128)(2,1)} %param.15, f32[256,3072]{1,0:T(8,128)S(1)} %fusion.48, f32[3072]{0:T(1024)S(1)} %bitcast.285, f32[256]{0:T(256)S(1)} %bitcast.296), kind=kOutput, calls=%fused_computation.50 | convolution fusion | flops 6448742400 | bytes 31994880 | tf_op jit(solution)/shard_map/dot_general | solution.py:24
  89.0 0.5 fusion.122
  89.5 12.7 %fusion.45 = bf16[256,4096]{1,0:T(8,128)(2,1)} fusion(bf16[256,3072]{1,0:T(8,128)(2,1)S(1)} %fusion.93, bf16[1,3072,4096]{2,1,0:T(8,128)(2,1)} %param.16, f32[4096]{0:T(1024)S(1)} %bitcast.277, f32[256]{0:T(256)S(1)} %broadcast_multiply_fusion.3), kind=kOutput, calls=%fused_computation.34 | convolution fusion | flops 6445596672 | bytes 28853248 | tf_op jit(solution)/shard_map/dot_general | solution.py:27
  102.2 6.4 %all-gather.8.cloned.1.call-done = bf16[256,4096]{1,0:T(8,128)(2,1)} async-done(((bf16[64,4096]{1,0:T(8,128)(2,1)}), bf16[256,4096]{1,0:T(8,128)(2,1)}) %all-gather.8.cloned.1.call-update) | async-done | bytes 2097168 | tf_op jit(solution)/shard_map/all_gather | solution.py:97
  108.7 2.2 convolution_multiply_fusion.2
  110.9 12.3 %fusion.51 = f32[256,3072]{1,0:T(8,128)S(1)} fusion(bf16[256,4096]{1,0:T(8,128)(2,1)} %all-gather.8.cloned.1.call-done, bf16[1,4096,3072]{2,1,0:T(8,128)(2,1)} %param.14, f32[3072]{0:T(1024)S(1)} %bitcast.279, f32[256]{0:T(256)S(1)} %bitcast.297), kind=kOutput, calls=%fused_computation.36 | convolution fusion | flops 6444023808 | bytes 30422016 | tf_op jit(solution)/shard_map/dot_general | solution.py:22
  123.3 12.1 %fusion.90 = bf16[256,3072]{1,0:T(8,128)(2,1)S(1)} fusion(bf16[256,4096]{1,0:T(8,128)(2,1)S(1)} %copy-done, bf16[1,4096,3072]{2,1,0:T(8,128)(2,1)} %param.15, f32[256,3072]{1,0:T(8,128)S(1)} %fusion.51, f32[3072]{0:T(1024)S(1)} %bitcast.281, f32[256]{0:T(256)S(1)} %bitcast.293), kind=kOutput, calls=%fused_computation.49 | convolution fusion | flops 6448742400 | bytes 31994880 | tf_op jit(solution)/shard_map/dot_general | solution.py:24
  135.4 0.5 fusion.118
  135.9 12.6 %fusion.42 = bf16[256,4096]{1,0:T(8,128)(2,1)} fusion(bf16[256,3072]{1,0:T(8,128)(2,1)S(1)} %fusion.90, bf16[1,3072,4096]{2,1,0:T(8,128)(2,1)} %param.16, f32[4096]{0:T(1024)S(1)} %bitcast.275, f32[256]{0:T(256)S(1)} %broadcast_multiply_fusion.2), kind=kOutput, calls=%fused_computation.33 | convolution fusion | flops 6445596672 | bytes 28853248 | tf_op jit(solution)/shard_map/dot_general | solution.py:27
  148.5 0.0 reduce-scatter.5.cloned.1.call-start
  148.6 0.1 copy.27
  148.7 0.1 convert_multiply_fusion.9
  148.8 0.1 convert_multiply_fusion.8
  148.9 0.1 fusion.130
  149.0 0.1 fusion.131
  149.2 0.0 all-gather.10.cloned.1.call-start
  149.3 12.6 %add_convert_fusion.1 = bf16[1024,3072]{1,0:T(8,128)(2,1)} fusion(f32[3072]{0:T(1024)S(1)} %bitcast.236, f32[1024]{0:T(1024)S(1)} %bitcast.268, f32[3072]{0:T(1024)S(1)} %bitcast.237, f32[1024]{0:T(1024)S(1)} %bitcast.269, f32[3072]{0:T(1024)S(1)} %bitcast.238, f32[1024]{0:T(1024)S(1)} %bitcast.270, f32[3072]{0:T(1024)S(1)} %bitcast.239, ...), kind=kLoop, calls=%fused_computation.25 | loop fusion | flops 62914560 | bytes 6422528 | tf_op jit(solution)/shard_map/convert_element_type | solution.py:44
  161.9 12.6 %add_convert_fusion.2 = bf16[1024,3072]{1,0:T(8,128)(2,1)} fusion(f32[3072]{0:T(1024)S(1)} %bitcast.233, f32[1024]{0:T(1024)S(1)} %bitcast.257, f32[3072]{0:T(1024)S(1)} %bitcast.232, f32[1024]{0:T(1024)S(1)} %bitcast.256, f32[3072]{0:T(1024)S(1)} %bitcast.231, f32[1024]{0:T(1024)S(1)} %bitcast.255, f32[3072]{0:T(1024)S(1)} %bitcast.230, ...), kind=kLoop, calls=%fused_computation.26 | loop fusion | flops 62914560 | bytes 6422528 | tf_op jit(solution)/shard_map/convert_element_type | solution.py:44
  174.5 16.6 %reduce-scatter.7.cloned.1.call-done = bf16[64,4096]{1,0:T(8,128)(2,1)} async-done(((bf16[256,4096]{1,0:T(8,128)(2,1)}), bf16[64,4096]{1,0:T(8,128)(2,1)}) %reduce-scatter.7.cloned.1.call-update) | async-done | bytes 524304 | tf_op jit(solution)/shard_map/reduce_scatter | solution.py:116
  191.1 1.6 fusion.111
  192.8 1.3 collective-permute-start.1
  194.1 42.1 %reduce-scatter.5.cloned.1.call-done = bf16[64,4096]{1,0:T(8,128)(2,1)} async-done(((bf16[256,4096]{1,0:T(8,128)(2,1)}), bf16[64,4096]{1,0:T(8,128)(2,1)}) %reduce-scatter.5.cloned.1.call-update) | async-done | bytes 524304 | tf_op jit(solution)/shard_map/reduce_scatter | solution.py:116
  236.1 1.6 fusion.107
  237.8 1.3 collective-permute-start
  239.1 10.3 %add_convert_fusion = bf16[3072,1024]{1,0:T(8,128)(2,1)} fusion(f32[1024]{0:T(1024)S(1)} %bitcast.260, f32[3072]{0:T(1024)S(1)} %bitcast.244, f32[1024]{0:T(1024)S(1)} %bitcast.261, f32[3072]{0:T(1024)S(1)} %bitcast.245, f32[1024]{0:T(1024)S(1)} %bitcast.262, f32[3072]{0:T(1024)S(1)} %bitcast.246, f32[1024]{0:T(1024)S(1)} %bitcast.263, ...), kind=kLoop, calls=%fused_computation.24 | loop fusion | flops 62914560 | bytes 6422528 | tf_op jit(solution)/shard_map/convert_element_type | solution.py:44
  249.4 0.2 fusion.100
  249.6 3.4 collective-permute-done
  252.9 0.2 fusion.96
  253.2 1.3 fusion.102
  254.5 0.0 all-gather.12.cloned.1.call-start
  254.5 0.5 all-gather.12.cloned.1.call-update
  255.1 0.0 reduce-scatter.9.cloned.1.call-start
  255.1 44.7 %all-gather.10.cloned.1.call-done = bf16[256,4096]{1,0:T(8,128)(2,1)} async-done(((bf16[64,4096]{1,0:T(8,128)(2,1)}), bf16[256,4096]{1,0:T(8,128)(2,1)}) %all-gather.10.cloned.1.call-update) | async-done | bytes 2097168 | tf_op jit(solution)/shard_map/all_gather | solution.py:97
  299.8 2.2 convolution_multiply_fusion.1
  302.1 15.7 %fusion.54 = f32[256,3072]{1,0:T(8,128)S(1)} fusion(bf16[256,4096]{1,0:T(8,128)(2,1)} %all-gather.10.cloned.1.call-done, bf16[1,4096,3072]{2,1,0:T(8,128)(2,1)} %param.14, f32[256]{0:T(256)S(1)} %bitcast.298, f32[3072]{0:T(1024)S(1)} %bitcast.284), kind=kOutput, calls=%fused_computation.37 | convolution fusion | flops 6444023808 | bytes 30422016 | tf_op jit(solution)/shard_map/dot_general | solution.py:22
  317.8 11.8 %fusion.87 = bf16[256,3072]{1,0:T(8,128)(2,1)S(1)} fusion(bf16[256,4096]{1,0:T(8,128)(2,1)S(1)} %copy-done.3, bf16[1,4096,3072]{2,1,0:T(8,128)(2,1)} %param.15, f32[256,3072]{1,0:T(8,128)S(1)} %fusion.54, f32[256]{0:T(256)S(1)} %bitcast.294, f32[3072]{0:T(1024)S(1)} %bitcast.286), kind=kOutput, calls=%fused_computation.48 | convolution fusion | flops 6448742400 | bytes 31994880 | tf_op jit(solution)/shard_map/dot_general | solution.py:24
  329.6 0.5 fusion.120
  330.1 12.7 %fusion.39 = bf16[256,4096]{1,0:T(8,128)(2,1)} fusion(bf16[256,3072]{1,0:T(8,128)(2,1)S(1)} %fusion.87, bf16[1,3072,4096]{2,1,0:T(8,128)(2,1)} %param.16, f32[256]{0:T(256)S(1)} %broadcast_multiply_fusion.1, f32[4096]{0:T(1024)S(1)} %bitcast.278), kind=kOutput, calls=%fused_computation.32 | convolution fusion | flops 6445596672 | bytes 28853248 | tf_op jit(solution)/shard_map/dot_general | solution.py:27
  342.8 3.5 all-gather.12.cloned.1.call-done
  346.4 2.2 convolution_multiply_fusion
  348.7 15.7 %fusion.57 = f32[256,3072]{1,0:T(8,128)S(1)} fusion(bf16[256,4096]{1,0:T(8,128)(2,1)} %all-gather.12.cloned.1.call-done, bf16[1,4096,3072]{2,1,0:T(8,128)(2,1)} %param.14, f32[256]{0:T(256)S(1)} %bitcast.299, f32[3072]{0:T(1024)S(1)} %bitcast.280), kind=kOutput, calls=%fused_computation.38 | convolution fusion | flops 6444023808 | bytes 30422016 | tf_op jit(solution)/shard_map/dot_general | solution.py:22
  364.4 11.9 %fusion.84 = bf16[256,3072]{1,0:T(8,128)(2,1)S(1)} fusion(bf16[256,4096]{1,0:T(8,128)(2,1)S(1)} %copy-done.2, bf16[1,4096,3072]{2,1,0:T(8,128)(2,1)} %param.15, f32[256,3072]{1,0:T(8,128)S(1)} %fusion.57, f32[256]{0:T(256)S(1)} %bitcast.295, f32[3072]{0:T(1024)S(1)} %bitcast.282), kind=kOutput, calls=%fused_computation.47 | convolution fusion | flops 6448742400 | bytes 31994880 | tf_op jit(solution)/shard_map/dot_general | solution.py:24
  376.3 0.5 fusion.116
  376.8 12.7 %fusion.36 = bf16[256,4096]{1,0:T(8,128)(2,1)} fusion(bf16[256,3072]{1,0:T(8,128)(2,1)S(1)} %fusion.84, bf16[1,3072,4096]{2,1,0:T(8,128)(2,1)} %param.16, f32[256]{0:T(256)S(1)} %broadcast_multiply_fusion, f32[4096]{0:T(1024)S(1)} %bitcast.276), kind=kOutput, calls=%fused_computation.31 | convolution fusion | flops 6445596672 | bytes 28853248 | tf_op jit(solution)/shard_map/dot_general | solution.py:27
  389.5 1.6 reduce-scatter.9.cloned.1.call-done
  391.1 1.2 fusion.115
  392.3 43.9 %reduce-scatter.11.cloned.1.call-done = bf16[64,4096]{1,0:T(8,128)(2,1)} async-done(((bf16[256,4096]{1,0:T(8,128)(2,1)}), bf16[64,4096]{1,0:T(8,128)(2,1)}) %reduce-scatter.11.cloned.1.call-update) | async-done | bytes 524304 | tf_op jit(solution)/shard_map/reduce_scatter | solution.py:116
  436.2 1.2 fusion.113
  437.5 0.1 maximum_bitcast_fusion
  437.6 2.1 copy.23
  (60 shorter events, 0.6 us)
Async XLA Ops:
  7.2 5.4 %copy-start.10 = (f32[1,4096]{1,0:T(1,128)S(1)}, f32[1,4096]{1,0:T(1,128)}, u32[]{:S(2)}) copy-start(f32[1,4096]{1,0:T(1,128)} %param.13) | copy-start | bytes 49156
  7.2 54.8 %all-gather.6.cloned.1.call-start = ((), (), s32[]{:S(2)}) async-start(), calls=%async_computation.4 | async-start | bytes 2621440 | tf_op jit(solution)/shard_map/all_gather | solution.py:97
  11.3 4.5 %copy-start.6 = (bf16[1,2,4096]{2,1,0:T(2,128)(2,1)S(1)}, bf16[1,2,4096]{2,1,0:T(2,128)(2,1)}, u32[]{:S(2)}) copy-start(bf16[1,2,4096]{2,1,0:T(2,128)(2,1)} %param.17) | copy-start | bytes 49156
  11.3 4.5 %copy-start.8 = (bf16[1,2,3072]{2,1,0:T(2,128)(2,1)S(1)}, bf16[1,2,3072]{2,1,0:T(2,128)(2,1)}, u32[]{:S(2)}) copy-start(bf16[1,2,3072]{2,1,0:T(2,128)(2,1)} %param.18) | copy-start | bytes 36868
  11.3 4.6 %copy-start.7 = (bf16[1,2,4096]{2,1,0:T(2,128)(2,1)S(1)}, bf16[1,2,4096]{2,1,0:T(2,128)(2,1)}, u32[]{:S(2)}) copy-start(bf16[1,2,4096]{2,1,0:T(2,128)(2,1)} %param.19) | copy-start | bytes 49156
  11.3 4.7 %copy-start.9 = (bf16[1,2,3072]{2,1,0:T(2,128)(2,1)S(1)}, bf16[1,2,3072]{2,1,0:T(2,128)(2,1)}, u32[]{:S(2)}) copy-start(bf16[1,2,3072]{2,1,0:T(2,128)(2,1)} %param.20) | copy-start | bytes 36868
  11.4 4.7 %copy-start.5 = (bf16[1,2,4096]{2,1,0:T(2,128)(2,1)S(1)}, bf16[1,2,4096]{2,1,0:T(2,128)(2,1)}, u32[]{:S(2)}) copy-start(bf16[1,2,4096]{2,1,0:T(2,128)(2,1)} %param.22) | copy-start | bytes 49156
  11.4 4.8 %copy-start.4 = (bf16[1,2,3072]{2,1,0:T(2,128)(2,1)S(1)}, bf16[1,2,3072]{2,1,0:T(2,128)(2,1)}, u32[]{:S(2)}) copy-start(bf16[1,2,3072]{2,1,0:T(2,128)(2,1)} %param.21) | copy-start | bytes 36868
  11.4 4.8 %copy-start.11 = (s32[2]{0:T(128)S(1)}, s32[2]{0:T(128)}, u32[]{:S(2)}) copy-start(s32[2]{0:T(128)} %param.23) | copy-start | bytes 28
  15.0 93.6 %all-gather.8.cloned.1.call-start = ((), (), s32[]{:S(2)}) async-start(), calls=%async_computation.5 | async-start | bytes 2621440 | tf_op jit(solution)/shard_map/all_gather | solution.py:97
  15.8 175.3 %reduce-scatter.7.cloned.1.call-start = ((), (), s32[]{:S(2)}) async-start(), calls=%async_computation.8 | async-start | bytes 2621440 | tf_op jit(solution)/shard_map/reduce_scatter | solution.py:116
  64.3 12.9 %copy-start.1 = (bf16[256,4096]{1,0:T(8,128)(2,1)S(1)}, bf16[256,4096]{1,0:T(8,128)(2,1)}, u32[]{:S(2)}) copy-start(bf16[256,4096]{1,0:T(8,128)(2,1)} %all-gather.6.cloned.1.call-done) | copy-start | bytes 6291460
  110.9 12.4 %copy-start = (bf16[256,4096]{1,0:T(8,128)(2,1)S(1)}, bf16[256,4096]{1,0:T(8,128)(2,1)}, u32[]{:S(2)}) copy-start(bf16[256,4096]{1,0:T(8,128)(2,1)} %all-gather.8.cloned.1.call-done) | copy-start | bytes 6291460
  148.5 87.6 %reduce-scatter.5.cloned.1.call-start = ((), (), s32[]{:S(2)}) async-start(), calls=%async_computation.6 | async-start | bytes 2621440 | tf_op jit(solution)/shard_map/reduce_scatter | solution.py:116
  149.2 150.6 %all-gather.10.cloned.1.call-start = ((), (), s32[]{:S(2)}) async-start(), calls=%async_computation.7 | async-start | bytes 2621440 | tf_op jit(solution)/shard_map/all_gather | solution.py:97
  192.8 56.6 %collective-permute-start.1 = (bf16[64,4096]{1,0:T(8,128)(2,1)S(1)}, bf16[64,4096]{1,0:T(8,128)(2,1)S(1)}, u32[]{:S(2)}, u32[]{:S(2)}) collective-permute-start(bf16[64,4096]{1,0:T(8,128)(2,1)S(1)} %fusion.111), channel_id=1, source_target_pairs={{0,1},{2,3},{4,5},{6,7},{8,9},{10,11},{12,13},{14,15},{16,17},{18,... | collective-permute-start | bytes 1572872 | tf_op jit(solution)/shard_map/ppermute | solution.py:123
  237.8 15.2 %collective-permute-start = (bf16[64,4096]{1,0:T(8,128)(2,1)S(1)}, bf16[64,4096]{1,0:T(8,128)(2,1)S(1)}, u32[]{:S(2)}, u32[]{:S(2)}) collective-permute-start(bf16[64,4096]{1,0:T(8,128)(2,1)S(1)} %fusion.107), channel_id=1, source_target_pairs={{0,1},{2,3},{4,5},{6,7},{8,9},{10,11},{12,13},{14,15},{16,17},{18,... | collective-permute-start | bytes 1572872 | tf_op jit(solution)/shard_map/ppermute | solution.py:123
  254.5 91.8 %all-gather.12.cloned.1.call-start = ((), (), s32[]{:S(2)}) async-start(), calls=%async_computation.9 | async-start | bytes 2621440 | tf_op jit(solution)/shard_map/all_gather | solution.py:97
  255.1 136.0 %reduce-scatter.9.cloned.1.call-start = ((), (), s32[]{:S(2)}) async-start(), calls=%async_computation.10 | async-start | bytes 2621440 | tf_op jit(solution)/shard_map/reduce_scatter | solution.py:116
  302.1 15.7 %copy-start.3 = (bf16[256,4096]{1,0:T(8,128)(2,1)S(1)}, bf16[256,4096]{1,0:T(8,128)(2,1)}, u32[]{:S(2)}) copy-start(bf16[256,4096]{1,0:T(8,128)(2,1)} %all-gather.10.cloned.1.call-done) | copy-start | bytes 6291460
  346.4 89.9 %reduce-scatter.11.cloned.1.call-start = ((), (), s32[]{:S(2)}) async-start(), calls=%async_computation.11 | async-start | bytes 2621440 | tf_op jit(solution)/shard_map/reduce_scatter | solution.py:116
  348.6 15.7 %copy-start.2 = (bf16[256,4096]{1,0:T(8,128)(2,1)S(1)}, bf16[256,4096]{1,0:T(8,128)(2,1)}, u32[]{:S(2)}) copy-start(bf16[256,4096]{1,0:T(8,128)(2,1)} %all-gather.12.cloned.1.call-done) | copy-start | bytes 6291460
Sparse Core Ops, SparseCore 0:
  15.1 46.8 all-gather.5
  64.2 44.4 all-gather.7
  148.6 42.4 reduce-scatter.6
  193.3 42.8 reduce-scatter.4
  254.6 45.1 all-gather.9
  301.8 44.4 all-gather.11
  348.6 42.4 reduce-scatter.8
  393.4 42.8 reduce-scatter.10
where the time goes:
time: 452 us; the launch traced here: 447 us
  waiting for transfers between devices  203 us (45%)
  matrix products  166 us (37%)
  other arithmetic  47 us (10%)
  between operations  14.8 us (3%)
  local copies, waits for them, and re-layouts  7.02 us (2%)
  blocking collectives  6.21 us (1%)
    reduce_scatter x4, waiting for transfers between devices, per_device(): summed = lax.psum_scatter(terms[k], 'tp', scatter_dimension=0, tiled=True)  104 us
    all_gather x4, waiting for transfers between devices, per_device(): pieces = [lax.all_gather(rows, 'tp', axis=0, tiled=True) for rows in normed]  94 us
    dot_general x4, matrix products, feed_forward(): gate = jnp.dot(piece, w_gate, preferred_element_type=jnp.float32)  56.6 us
    dot_general x4, matrix products, feed_forward(): term = jnp.dot(inner, w_down, preferred_element_type=jnp.float32)  50.7 us
    dot_general x4, matrix products, feed_forward(): upper = jnp.dot(piece, w_up, preferred_element_type=jnp.float32)  47.6 us
    convert_element_type x3, other arithmetic, grouped_outer(): return total.astype(jnp.bfloat16)  35.5 us
  transfers between devices with their start and end apart: 10, of which 9 were waited for; matrix products, arithmetic and copies ran while one was open for 37% of the time, Pallas kernels for 0%

commit v1 on v0

v1 whole, which is shorter than its diff:
```python
import functools
import math

import jax
import jax.numpy as jnp
from jax import lax
from jax.experimental import pallas as pl
from jax.experimental.pallas import tpu as pltpu
from jax.sharding import PartitionSpec as P

MESH = pl.DeviceIdType.MESH
f32, bf16 = jnp.float32, jnp.bfloat16

sigma_scale = 0.3
norm_eps = 1e-05

ROWS = 32
HOP_TICKS = 4
GATHER_TICKS = 4
VMEM_BYTES = 66_000_000


def widths(D, F):
    hidden = next(w for w in (256, 128) if F % w == 0)
    columns = next(w for w in (512, 256, 128) if D % w == 0 and D // w >= 4)
    return hidden, columns


def relay_kernel(
    dims,
    x_hbm, wg_hbm, wu_hbm, wd_hbm, gain, lefts, gr, ur, dl, dr, vec,
    out_hbm, every_hbm,
    xh, nb, hid, part, rr, ll, xo, acc, side_g, side_u, side_d, wg, wu, wd, ve,
    w_sem, wd_sem, hop_recv, hop_send, out_sem,
    ag_recv, ag_right, ag_left, rr_recv, rr_send, ll_recv, ll_send,
    v_send, v_recv, v_out,
):
    n, T, S, Pn, members, D, F, HB, DB, keep, ring, dring = dims
    J, Nd, M = F // HB, D // DB, T * ROWS
    me, s, p = lax.axis_index("tp"), lax.axis_index("pp"), lax.axis_index("pop")
    coef_in = sigma_scale / math.sqrt(D)
    coef_hidden = sigma_scale / math.sqrt(F * T)
    has_left, has_right = me > 0, me < T - 1
    has_prev, has_next = s > 0, s < S - 1
    stream = J - keep

    def gu_copies(j, slot):
        cols = pl.ds(pl.multiple_of(j * HB, HB), HB)
        return (
            pltpu.make_async_copy(wg_hbm.at[:, cols], wg.at[slot], w_sem.at[slot, 0]),
            pltpu.make_async_copy(wu_hbm.at[:, cols], wu.at[slot], w_sem.at[slot, 1]),
        )

    def wd_copy(b, slot):
        cols = pl.ds(pl.multiple_of(b * DB, DB), DB)
        return pltpu.make_async_copy(wd_hbm.at[:, cols], wd.at[slot], wd_sem.at[slot])

    def start(copies):
        for copy in copies:
            copy.start()

    def own_copy(c, b):
        cols = pl.ds(pl.multiple_of(b * DB, DB), DB)
        return pltpu.make_async_copy(x_hbm.at[c, :, cols], xh.at[c, :, cols], hop_recv.at[c, b])

    def each(count, body):
        lax.fori_loop(0, count, lambda i, z: (body(i), z)[1], 0)

    def between(lo, hi, body):
        lax.fori_loop(lo, hi, lambda i, z: (body(i), z)[1], 0)

    @pl.when(s == 0)
    def _():
        each(n, lambda c: each(Nd, lambda b: own_copy(c, b).start()))

    for j in range(keep + ring):
        start(gu_copies(j, j))
    for b in range(dring):
        wd_copy(b, b).start()

    barrier = pltpu.get_barrier_semaphore()

    def greet(cond, device):
        @pl.when(cond)
        def _():
            pl.semaphore_signal(barrier, inc=1, device_id=device, device_id_type=MESH)

    greet(has_left, {"tp": me - 1})
    greet(has_right, {"tp": me + 1})
    greet(has_prev, {"pp": s - 1})
    greet(has_next, {"pp": s + 1})
    for k in range(1, Pn):
        pl.semaphore_signal(barrier, inc=1, device_id={"pop": lax.rem(p + k, Pn)}, device_id_type=MESH)
    as_int = lambda v: v.astype(jnp.int32)
    pl.semaphore_wait(barrier, as_int(has_left) + as_int(has_right) + as_int(has_prev) + as_int(has_next) + Pn - 1)

    def vec_copy(k):
        return pltpu.make_async_remote_copy(
            src_ref=vec, dst_ref=ve.at[k - 1], send_sem=v_send.at[k - 1], recv_sem=v_recv.at[k - 1],
            device_id={"pop": lax.rem(p + k, Pn)}, device_id_type=MESH,
        )

    def ag_copy(c, o, right):
        return pltpu.make_async_remote_copy(
            src_ref=nb.at[c, o], dst_ref=nb.at[c, o],
            send_sem=(ag_right if right else ag_left).at[c, o], recv_sem=ag_recv.at[c, o],
            device_id={"tp": me + 1 if right else me - 1}, device_id_type=MESH,
        )

    def ag_send(c, o, cond, right):
        @pl.when(cond)
        def _():
            ag_copy(c, o, right).start()

    def normalize(c):
        total = jnp.zeros((ROWS, 1), f32)
        for b in range(Nd):
            own_copy(c, b).wait()
            values = xh[c, :, b * DB : (b + 1) * DB].astype(f32)
            total = total + jnp.sum(values * values, axis=-1, keepdims=True)
        scale = lax.rsqrt(total / D + norm_eps)
        for b in range(Nd):
            cols = slice(b * DB, (b + 1) * DB)
            values = xh[c, :, cols].astype(f32)
            nb[c, me, :, cols] = (values * scale * gain[:, cols]).astype(bf16)
        ag_send(c, me, has_right, True)
        ag_send(c, me, has_left, False)

    def ag_step(c, k):
        @pl.when(k == 0)
        def _():
            normalize(c)

        @pl.when(jnp.logical_and(k > 0, me - k >= 0))
        def _():
            o = me - k
            ag_copy(c, o, True).wait_recv()
            ag_send(c, o, has_right, True)

        @pl.when(jnp.logical_and(k > 0, me + k < T))
        def _():
            o = me + k
            ag_copy(c, o, False).wait_recv()
            ag_send(c, o, has_left, False)

    def sum_copy(c, b, o, right):
        buf = rr if right else ll
        return pltpu.make_async_remote_copy(
            src_ref=buf.at[c, b, o], dst_ref=buf.at[c, b, o],
            send_sem=(rr_send if right else ll_send).at[c, b, o],
            recv_sem=(rr_recv if right else ll_recv).at[c, b, o],
            device_id={"tp": me + 1 if right else me - 1}, device_id_type=MESH,
        )

    def pass_on(c, b, right):
        buf = rr if right else ll
        first = jnp.logical_not(has_left if right else has_right)

        def one(o):
            @pl.when(first)
            def _():
                buf[c, b, o] = part[b, o]

            @pl.when(jnp.logical_not(first))
            def _():
                sum_copy(c, b, o, right).wait_recv()
                buf[c, b, o] = (buf[c, b, o].astype(f32) + part[b, o].astype(f32)).astype(bf16)

            sum_copy(c, b, o, right).start()

        if right:
            between(me + 1, T, one)
        else:
            between(0, me, one)

    def hop_copy(c, b):
        cols = pl.ds(pl.multiple_of(b * DB, DB), DB)
        return pltpu.make_async_remote_copy(
            src_ref=xo.at[c, :, cols], dst_ref=xh.at[c, :, cols],
            send_sem=hop_send.at[c, b], recv_sem=hop_recv.at[c, b],
            device_id={"pp": s + 1}, device_id_type=MESH,
        )

    def out_copy(c, b):
        cols = pl.ds(pl.multiple_of(b * DB, DB), DB)
        return pltpu.make_async_copy(xo.at[c, :, cols], out_hbm.at[c, :, cols], out_sem.at[c, b])

    def finish(c, b):
        cols = pl.ds(pl.multiple_of(b * DB, DB), DB)
        acc[...] = part[b, me].astype(f32)

        @pl.when(has_left)
        def _():
            sum_copy(c, b, me, True).wait_recv()
            acc[...] += rr[c, b, me].astype(f32)

        @pl.when(has_right)
        def _():
            sum_copy(c, b, me, False).wait_recv()
            acc[...] += ll[c, b, me].astype(f32)

        xo[c, :, cols] = (xh[c, :, cols].astype(f32) + acc[...]).astype(bf16)
        out_copy(c, b).start()

        @pl.when(has_next)
        def _():
            hop_copy(c, b).start()

    last_hop = jnp.maximum(me, T - 1 - me)

    def rs_step(c, i):
        def at(lag, body):
            b = i - lag * HOP_TICKS

            @pl.when(jnp.logical_and(b >= 0, b < Nd))
            def _():
                body(b)

        at(me, lambda b: pass_on(c, b, True))
        at(T - 1 - me, lambda b: pass_on(c, b, False))
        at(last_hop, lambda b: finish(c, b))

    rs_steps = Nd + (T - 1) * HOP_TICKS
    spill = -(-(rs_steps - Nd) // J)

    ticks = J + Nd
    begin = jnp.where(s == 0, 1, 8)

    def gathered(tick):
        done = jnp.clip((tick - begin + GATHER_TICKS) // GATHER_TICKS, 0, T)
        return jnp.where(tick >= ticks - 1, T, done)

    def communicate(c, tick):
        @pl.when(c + 1 < n)
        def _():
            lo = jnp.where(tick == 0, 0, gathered(tick - 1))
            between(lo, gathered(tick), lambda k: ag_step(c + 1, k))

    def member_side(sides, first):
        member = lax.broadcasted_iota(jnp.int32, sides.shape, 0) % members + first
        column = lax.broadcasted_iota(jnp.int32, sides.shape, 1)
        return jnp.sum(jnp.where(member == column, sides, 0.0), axis=1, keepdims=True)

    def add_side(product, side, right):
        wide = product.reshape(T, ROWS, product.shape[-1])
        wide = wide + side[...].reshape(T, ROWS, 1) * right.astype(f32)[None]
        return wide.reshape(product.shape)

    NT = (((1,), (1,)), ((), ()))

    each(T, lambda k: ag_step(0, k))
    for k in range(1, Pn):
        vec_copy(k).start()

    def chunk(c):
        rows = lambda: nb[c].reshape(M, D)
        sides = coef_in * lax.dot_general(rows(), lefts[...], NT, preferred_element_type=f32)
        side_g[...] = member_side(sides, 0)
        side_u[...] = member_side(sides, members)

        def gu(j):
            if stream:
                q = c * stream + j - keep
                slot = jnp.where(j < keep, j, keep + (q + ring) % ring)
            else:
                q, slot = 0, j

            @pl.when(jnp.logical_or(c == 0, j >= keep))
            def _():
                for copy in gu_copies(j, slot):
                    copy.wait()

            cols = pl.ds(pl.multiple_of(j * HB, HB), HB)
            x = rows()
            gate = jnp.dot(x, wg[slot], preferred_element_type=f32)
            upper = jnp.dot(x, wu[slot], preferred_element_type=f32)
            gate = add_side(gate, side_g, gr[:, cols])
            upper = add_side(upper, side_u, ur[:, cols])
            hid[:, cols] = (gate / (1.0 + jnp.exp(-gate)) * upper).astype(bf16)
            if stream:
                ahead = q + ring

                @pl.when(jnp.logical_and(j >= keep, ahead < n * stream))
                def _():
                    start(gu_copies(keep + ahead % stream, slot))

            @pl.when(c > 0)
            def _():
                between(Nd + j * spill, jnp.minimum(Nd + (j + 1) * spill, rs_steps), lambda i: rs_step(c - 1, i))

            communicate(c, j)

        each(J, gu)
        side_d[...] = member_side(coef_hidden * lax.dot_general(hid[...], dl[...], NT, preferred_element_type=f32), 0)

        def down(b):
            q = c * Nd + b
            slot = q % dring
            cols = pl.ds(pl.multiple_of(b * DB, DB), DB)
            wd_copy(b, slot).wait()
            term = jnp.dot(hid[...], wd[slot], preferred_element_type=f32)
            part[b] = add_side(term, side_d, dr[:, cols]).astype(bf16).reshape(T, ROWS, DB)

            @pl.when(q + dring < n * Nd)
            def _():
                wd_copy((b + dring) % Nd, slot).start()

            rs_step(c, b)
            communicate(c, J + b)

        each(Nd, down)

    each(n, chunk)
    between(Nd, rs_steps, lambda i: rs_step(n - 1, i))

    out_own = pltpu.make_async_copy(vec, every_hbm.at[p], v_out.at[Pn - 1])
    out_own.start()
    for k in range(1, Pn):
        vec_copy(k).wait()
        pltpu.make_async_copy(ve.at[k - 1], every_hbm.at[lax.rem(p + Pn - k, Pn)], v_out.at[k - 1]).start()

    def drain(c):
        def gather(o):
            @pl.when(jnp.logical_and(has_right, o <= me))
            def _():
                ag_copy(c, o, True).wait_send()

            @pl.when(jnp.logical_and(has_left, o >= me))
            def _():
                ag_copy(c, o, False).wait_send()

        each(T, gather)

        def block(b):
            between(me + 1, T, lambda o: sum_copy(c, b, o, True).wait_send())
            between(0, me, lambda o: sum_copy(c, b, o, False).wait_send())
            out_copy(c, b).wait()

            @pl.when(has_next)
            def _():
                hop_copy(c, b).wait_send()

        each(Nd, block)

    each(n, drain)
    out_own.wait()
    for k in range(1, Pn):
        pltpu.make_async_copy(ve.at[k - 1], every_hbm.at[lax.rem(p + Pn - k, Pn)], v_out.at[k - 1]).wait()


def relay(x, w_gate, w_up, w_down, gain, lefts, gr, ur, dl, dr, vec, members):
    n, _, D = x.shape
    F = w_gate.shape[1]
    T, S, Pn = (lax.axis_size(a) for a in ("tp", "pp", "pop"))
    HB, DB = widths(D, F)
    J, Nd, M = F // HB, D // DB, T * ROWS
    dring = min(3, Nd)
    fixed = 2 * (3 * n * ROWS * D + n * M * D + M * F + M * D + 2 * n * M * D + dring * F * DB) + 6_000_000
    slots = min(J, (VMEM_BYTES - fixed) // (4 * D * HB))
    ring = 0 if slots == J else min(3, slots)
    keep = slots - ring
    dims = (n, T, S, Pn, members, D, F, HB, DB, keep, ring, dring)
    vmem, hbm = pl.BlockSpec(memory_space=pltpu.VMEM), pl.BlockSpec(memory_space=pl.ANY)
    dma = pltpu.SemaphoreType.DMA
    return pl.pallas_call(
        functools.partial(relay_kernel, dims),
        out_shape=(
            jax.ShapeDtypeStruct((n, ROWS, D), bf16),
            jax.ShapeDtypeStruct((Pn,) + vec.shape, bf16),
        ),
        in_specs=[hbm] * 4 + [vmem] * 7,
        out_specs=(hbm, hbm),
        scratch_shapes=[
            pltpu.VMEM((n, ROWS, D), bf16),
            pltpu.VMEM((n, T, ROWS, D), bf16),
            pltpu.VMEM((M, F), bf16),
            pltpu.VMEM((Nd, T, ROWS, DB), bf16),
            pltpu.VMEM((n, Nd, T, ROWS, DB), bf16),
            pltpu.VMEM((n, Nd, T, ROWS, DB), bf16),
            pltpu.VMEM((n, ROWS, D), bf16),
            pltpu.VMEM((ROWS, DB), f32),
            pltpu.VMEM((M, 1), f32),
            pltpu.VMEM((M, 1), f32),
            pltpu.VMEM((M, 1), f32),
            pltpu.VMEM((slots, D, HB), bf16),
            pltpu.VMEM((slots, D, HB), bf16),
            pltpu.VMEM((dring, F, DB), bf16),
            pltpu.VMEM((Pn - 1,) + vec.shape, bf16),
            dma((slots, 2)),
            dma((dring,)),
            dma((n, Nd)),
            dma((n, Nd)),
            dma((n, Nd)),
            dma((n, T)),
            dma((n, T)),
            dma((n, T)),
            dma((n, Nd, T)),
            dma((n, Nd, T)),
            dma((n, Nd, T)),
            dma((n, Nd, T)),
            dma((Pn - 1,)),
            dma((Pn - 1,)),
            dma((Pn,)),
        ],
        compiler_params=pltpu.CompilerParams(collective_id=0, has_side_effects=True, vmem_limit_bytes=67_000_000),
    )(x, w_gate, w_up, w_down, gain, lefts, gr, ur, dl, dr, vec)


def low_rank(left, right, fitness):
    weighted = fitness[:, None] * left.astype(f32)
    high = lax.reduce_precision(weighted, 8, 7)
    both = jnp.concatenate([high, weighted - high]).astype(bf16)
    return jnp.einsum("pi,pj->ij", both, jnp.concatenate([right, right]), preferred_element_type=f32).astype(bf16)


def per_device(
    hidden_in, norm_gain, w_gate, w_up, w_down,
    gate_left, gate_right, up_left, up_right, down_left, down_right, ranks,
):
    tokens, members, D = hidden_in.shape
    F = w_gate.shape[2]
    Pn = lax.axis_size("pop")
    n = tokens * members // ROWS
    x = hidden_in.reshape(n, ROWS, D)

    def rows16(*vectors):
        stacked = jnp.concatenate(vectors)
        return jnp.pad(stacked, ((0, -stacked.shape[0] % 16), (0, 0)))

    def expand(vectors):
        return jnp.tile(vectors, (ROWS // members, 1))

    vectors = [gate_left[0], gate_right[0], up_left[0], up_right[0], down_left[0], down_right[0]]
    column = jnp.broadcast_to(ranks.astype(bf16)[:, None], (members, 128))
    pieces = [v.reshape(-1, 128) for v in vectors + [column]]
    lengths = [piece.shape[0] for piece in pieces]
    packed = rows16(*pieces)

    out, everyone = relay(
        x, w_gate[0], w_up[0], w_down[0], norm_gain,
        rows16(gate_left[0], up_left[0]), expand(gate_right[0]), expand(up_right[0]),
        rows16(down_left[0]), expand(down_right[0]), packed, members,
    )

    population = members * Pn
    ends = [sum(lengths[: i + 1]) for i in range(len(lengths))]
    gl, gr, ul, ur, dl, dr, rank = [
        everyone[:, end - length : end].reshape(population, -1) for end, length in zip(ends, lengths)
    ]
    fitness = (2.0 * rank[:, 0].astype(f32) / (population - 1) - 1.0) / math.sqrt(population)
    share_size = D // Pn
    first = lax.axis_index("pop") * share_size

    def share(full):
        return lax.dynamic_slice_in_dim(full, first, share_size, 1)

    return (
        out.reshape(1, tokens, members, D),
        low_rank(share(gl), gr, fitness)[None],
        low_rank(share(ul), ur, fitness)[None],
        low_rank(dl, share(dr), fitness)[None],
    )


def solution(mesh):
    placed = (
        P("tp", "pop", None),
        P("pp", None),
        P("pp", None, "tp"),
        P("pp", None, "tp"),
        P("pp", "tp", None),
        P("pp", "pop", None),
        P("pp", "pop", "tp"),
        P("pp", "pop", None),
        P("pp", "pop", "tp"),
        P("pp", "pop", "tp"),
        P("pp", "pop", None),
        P("pop"),
    )
    return jax.shard_map(
        per_device,
        mesh=mesh,
        in_specs=placed,
        out_specs=(
            P("pp", "tp", "pop", None),
            P("pp", "pop", "tp"),
            P("pp", "pop", "tp"),
            P("pp", "tp", "pop"),
        ),
        check_vma=False,
    )
```

time: 452 us -> 260 us (0.58)
  Pallas kernels: 0 us -> 221 us
  waiting for transfers between devices: 203 us -> 0 us
  matrix products: 166 us -> 13.6 us
  other arithmetic: 47 us -> 3.13 us
  between operations: 14.8 us -> 0.76 us
  local copies, waits for them, and re-layouts: 7.02 us -> 18 us
  blocking collectives: 6.21 us -> 0 us
    pallas_call x0 -> x1, Pallas kernels: none -> 221 us  [relay(): pl.pallas_call(functools.partial(relay_kernel, dims), out_shape=(jax.Shap...]
    dot_general x20 -> x3, matrix products: 166 us -> 13.6 us  [low_rank(): jnp.einsum('pi,pj->ij', both, jnp.concatenate([right, right]), preferred_...]
    reduce_scatter x4 -> x0, waiting for transfers between devices: 104 us -> none  [per_device(): summed = lax.psum_scatter(terms[k], 'tp', scatter_dimension=0, tiled=True)]
    all_gather x4 -> x0, waiting for transfers between devices: 94 us -> none  [per_device(): pieces = [lax.all_gather(rows, 'tp', axis=0, tiled=True) for rows in normed]]
    convert_element_type x13 -> x2, other arithmetic: 42.6 us -> 1.53 us  [the longest x1 0.87 us: low_rank(): weighted = fitness[:, None] * left.astype(f32)]
    another operation x1 -> x12, local copies, waits for them, and re-layouts: 0.05 us -> 9.23 us  [the longest x6 4.85 us: expand(): return jnp.tile(vectors, (ROWS // members, 1))]
    all_gather x1 -> x0, blocking collectives: 6.21 us -> none  [low_rank_updates(): everyone = lax.all_gather(packed, 'pop', axis=0, tiled=True)]
    reshape x0 -> x7, local copies, waits for them, and re-layouts: none -> 4.92 us  [the longest x1 2.53 us: per_device(): out.reshape(1, tokens, members, D)]
  transfers between devices with their start and end apart: 10 -> 0, of which waited for: 9 -> 0; matrix products, arithmetic and copies ran while one was open for 37% -> 0% of each run, Pallas kernels for 0% -> 0%
where the time goes in v1:
time: 260 us; the launch traced here: 256 us
  Pallas kernels  221 us (85%)
  local copies, waits for them, and re-layouts  18 us (7%)
  matrix products  13.6 us (5%)
  other arithmetic  3.13 us (1%)
    pallas_call x1, Pallas kernels, relay(): pl.pallas_call(functools.partial(relay_kernel, dims), out_shape=(jax.Shap...  221 us
    dot_general x3, matrix products, low_rank(): jnp.einsum('pi,pj->ij', both, jnp.concatenate([right, right]), preferred_...  13.6 us

profile of v1, /device:TPU:6, one launch (start us, length us, event | category | flops | bytes accessed | tf_op | source)
XLA Modules:
  0.0 256.2 jit_solution(5871112797169190008)
XLA Ops:
  0.6 0.7 convert_element_type.37
  1.3 0.7 reshape_squeeze.19
  2.0 0.7 reshape_squeeze.21
  2.7 0.7 reshape_squeeze.22
  3.5 0.7 reshape_squeeze.18
  4.2 0.7 reshape_squeeze.20
  4.9 0.7 reshape_squeeze.23
  5.8 0.1 constant_dynamic-update-slice_fusion
  5.8 0.7 pad.14.vec
  6.5 1.4 pad.13.dl
  7.9 1.4 fusion.2.lefts
  9.3 0.8 tile.34
  10.1 0.8 tile.35.ur
  10.8 0.8 tile.31
  11.7 0.8 tile.32.gr
  12.4 0.9 tile.37
  13.3 0.8 tile.38.dr
  14.1 2.2 reshape.48.x_hbm
  16.4 220.7 %shard_map.147 = (bf16[4,32,4096]{2,1,0:T(8,128)(2,1)}, bf16[4,352,128]{2,1,0:T(8,128)(2,1)}) custom-call(bf16[4,32,4096]{2,1,0:T(8,128)(2,1)} %reshape.48.x_hbm, bf16[4096,3072]{1,0:T(8,128)(2,1)} %bitcast.17, bf16[4096,3072]{1,0:T(8,128)(2,1)} %bitcast.18, bf16[3072,4096]{1,0:T(8,128)(2,1)} %bitcast.19, f32[1,4096]{1,0:T(1,128)} %gain.1, ...), custom_call_target="tpu_custom_call" | custom-call | tf_op jit(solution)/shard_map/pallas_call | solution.py:365
  237.0 2.5 reshape.49
  239.6 0.7 slice.24
  240.3 0.1 copy.18
  240.4 0.9 fusion.27
  241.3 0.9 slice_convert_fusion
  242.2 0.1 reduce-precision_convert_fusion
  242.5 0.1 reduce-precision_convert_fusion.1
  242.6 4.5 %convert_bitcast_fusion = bf16[1,3072,1024]{2,1,0:T(8,128)(2,1)} fusion(bf16[8,3072]{1,0:T(8,128)(2,1)S(1)} %get-tuple-element.15, bf16[8,3072]{1,0:T(8,128)(2,1)S(1)} %get-tuple-element.14, bf16[8,1024]{1,0:T(8,128)(2,1)S(1)} %constant_dynamic-slice_fusion), kind=kOutput, calls=%fused_computation | convolution fusion | flops 104071168 | bytes 6406144 | tf_op jit(solution)/shard_map/pi,pj->ij/dot_general | solution.py:413
  247.1 4.5 %convert_bitcast_fusion.1 = bf16[1,1024,3072]{2,1,0:T(8,128)(2,1)} fusion(bf16[8,3072]{1,0:T(8,128)(2,1)S(1)} %reshape.54, bf16[8,1024]{1,0:T(8,128)(2,1)S(1)} %get-tuple-element.17, bf16[8,1024]{1,0:T(8,128)(2,1)S(1)} %get-tuple-element.16), kind=kOutput, calls=%fused_computation.1 | convolution fusion | flops 104071168 | bytes 6373376 | tf_op jit(solution)/shard_map/pi,pj->ij/dot_general | solution.py:413
  251.6 4.5 %convert_bitcast_fusion.2 = bf16[1,1024,3072]{2,1,0:T(8,128)(2,1)} fusion(bf16[8,3072]{1,0:T(8,128)(2,1)S(1)} %reshape.52, bf16[8,1024]{1,0:T(8,128)(2,1)S(1)} %get-tuple-element.20, bf16[8,1024]{1,0:T(8,128)(2,1)S(1)} %get-tuple-element.21), kind=kOutput, calls=%fused_computation.2 | convolution fusion | flops 104071168 | bytes 6373376 | tf_op jit(solution)/shard_map/pi,pj->ij/dot_general | solution.py:413
  (14 shorter events, 0.2 us)

commit v2 on v1

v2 whole, which is shorter than its diff:
```python
import functools
import math

import jax
import jax.numpy as jnp
from jax import lax
from jax.experimental import pallas as pl
from jax.experimental.pallas import tpu as pltpu
from jax.sharding import PartitionSpec as P

MESH = pl.DeviceIdType.MESH
f32, bf16 = jnp.float32, jnp.bfloat16

sigma_scale = 0.3
norm_eps = 1e-05

ROWS = 32
HOP_TICKS = 4
GATHER_TICKS = 2
FIRST_BEGIN = 1
LATER_BEGIN = 3
VMEM_BYTES = 66_000_000
RESERVE = 1_500_000


def widths(D, F):
    hidden = next(w for w in (256, 128) if F % w == 0)
    columns = next(w for w in (512, 256, 128) if D % w == 0 and D // w >= 4)
    return hidden, columns


def relay_kernel(
    dims,
    x_hbm, wg_hbm, wu_hbm, wd_hbm, gain, gl, gr, ul, ur, dl, dr, fit, token,
    out_hbm, egl, egr, eul, eur, edl, edr, efit,
    gx, xn, hid, part, rr, ll, xo, acc, side_g, side_u, side_d, wg, wu, wd, stack, lefts, downs,
    w_sem, wd_sem, hop_recv, hop_send, out_sem,
    ag_recv, ag_right, ag_left, rr_recv, rr_send, ll_recv, ll_send,
    v_send, v_recv, v_own, ready,
):
    n, T, S, Pn, members, D, F, HB, DB, keep, ring, dring = dims
    J, Nd, M = F // HB, D // DB, T * ROWS
    G = Nd // 2 if Nd % 2 == 0 else Nd
    GW = D // G
    me, s, p = lax.axis_index("tp"), lax.axis_index("pp"), lax.axis_index("pop")
    coef_in = sigma_scale / math.sqrt(D)
    coef_hidden = sigma_scale / math.sqrt(F * T)
    has_left, has_right = me > 0, me < T - 1
    has_prev, has_next = s > 0, s < S - 1
    stream = J - keep

    def gu_copies(j, slot):
        cols = pl.ds(pl.multiple_of(j * HB, HB), HB)
        return (
            pltpu.make_async_copy(wg_hbm.at[:, cols], wg.at[slot], w_sem.at[slot, 0]),
            pltpu.make_async_copy(wu_hbm.at[:, cols], wu.at[slot], w_sem.at[slot, 1]),
        )

    def wd_copy(b, slot):
        cols = pl.ds(pl.multiple_of(b * DB, DB), DB)
        return pltpu.make_async_copy(wd_hbm.at[:, cols], wd.at[slot], wd_sem.at[slot])

    def start(copies):
        for copy in copies:
            copy.start()

    def own_copy(c, b):
        cols = pl.ds(pl.multiple_of(b * DB, DB), DB)
        return pltpu.make_async_copy(x_hbm.at[c, :, cols], gx.at[c, me, :, cols], hop_recv.at[c, b])

    def each(count, body):
        lax.fori_loop(0, count, lambda i, z: (body(i), z)[1], 0)

    def between(lo, hi, body):
        lax.fori_loop(lo, hi, lambda i, z: (body(i), z)[1], 0)

    @pl.when(s == 0)
    def _():
        each(n, lambda c: each(Nd, lambda b: own_copy(c, b).start()))

    for j in range(keep + ring):
        start(gu_copies(j, j))
    for b in range(dring):
        wd_copy(b, b).start()

    barrier = pltpu.get_barrier_semaphore()

    def greet(cond, device):
        @pl.when(cond)
        def _():
            pl.semaphore_signal(barrier, inc=1, device_id=device, device_id_type=MESH)

    greet(has_left, {"tp": me - 1})
    greet(has_right, {"tp": me + 1})
    greet(has_next, {"pp": s + 1})
    for k in range(1, Pn):
        pl.semaphore_signal(barrier, inc=1, device_id={"pop": lax.rem(p + k, Pn)}, device_id_type=MESH)
    as_int = lambda v: v.astype(jnp.int32)
    pl.semaphore_wait(barrier, as_int(has_left) + as_int(has_right) + as_int(has_prev) + Pn - 1)

    @pl.when(has_prev)
    def _():
        pl.semaphore_signal(ready, inc=1, device_id={"pp": s - 1}, device_id_type=MESH)

    vectors = Exchange((gl, gr, ul, ur, dl, dr, fit), (egl, egr, eul, eur, edl, edr, efit), v_send, v_recv, v_own, p, Pn)

    def side_rows(first, second, target):
        width = target.shape[1]
        stack[...] = jnp.zeros_like(stack)
        stack[0:members, 0:width] = first[...].astype(f32)
        if second is not None:
            stack[members : 2 * members, 0:width] = second[...].astype(f32)
        target[...] = stack[:, 0:width].astype(bf16)

    def ag_copy(c, g, o, right):
        cols = pl.ds(pl.multiple_of(g * GW, GW), GW)
        return pltpu.make_async_remote_copy(
            src_ref=gx.at[c, o, :, cols], dst_ref=gx.at[c, o, :, cols],
            send_sem=(ag_right if right else ag_left).at[c, g, o], recv_sem=ag_recv.at[c, g, o],
            device_id={"tp": me + 1 if right else me - 1}, device_id_type=MESH,
        )

    def ag_send(c, g, o, cond, right):
        @pl.when(cond)
        def _():
            ag_copy(c, g, o, right).start()

    def ag_own(c, g):
        for u in range(GW // DB):
            own_copy(c, g * (GW // DB) + u).wait()
        ag_send(c, g, me, has_right, True)
        ag_send(c, g, me, has_left, False)

    def ag_pass(c, g, k):
        @pl.when(me - k >= 0)
        def _():
            ag_copy(c, g, me - k, True).wait_recv()
            ag_send(c, g, me - k, has_right, True)

        @pl.when(me + k < T)
        def _():
            ag_copy(c, g, me + k, False).wait_recv()
            ag_send(c, g, me + k, has_left, False)

    waves = G + T - 1

    def ag_step(c, w):
        @pl.when(w < G)
        def _():
            ag_own(c, w)

        between(jnp.maximum(1, w - G + 1), jnp.minimum(w, T - 1) + 1, lambda k: ag_pass(c, w - k, k))

    def normalize(c, t):
        total = jnp.zeros((ROWS, 1), f32)
        for b in range(Nd):
            values = gx[c, t, :, b * DB : (b + 1) * DB].astype(f32)
            total = total + jnp.sum(values * values, axis=-1, keepdims=True)
        scale = lax.rsqrt(total / D + norm_eps)
        for b in range(Nd):
            cols = slice(b * DB, (b + 1) * DB)
            values = gx[c, t, :, cols].astype(f32)
            xn[pl.ds(pl.multiple_of(t * ROWS, ROWS), ROWS), cols] = (values * scale * gain[:, cols]).astype(bf16)

    def sum_copy(c, b, k, right):
        buf, blocks = (rr, pl.ds(k + 1, T - 1 - k)) if right else (ll, pl.ds(0, k))
        return pltpu.make_async_remote_copy(
            src_ref=buf.at[c, b, blocks], dst_ref=buf.at[c, b, blocks],
            send_sem=(rr_send if right else ll_send).at[c, b],
            recv_sem=(rr_recv if right else ll_recv).at[c, b],
            device_id={"tp": me + 1 if right else me - 1}, device_id_type=MESH,
        )

    def senders(right):
        return range(T - 1) if right else range(1, T)

    def pass_on(c, b, right):
        buf = rr if right else ll
        for k in senders(right):
            first = k == (0 if right else T - 1)
            lo, hi = (k + 1, T) if right else (0, k)

            @pl.when(me == k)
            def _():
                if first:
                    merge = lambda at: part[b, at]
                else:
                    sum_copy(c, b, k - 1 if right else k + 1, right).wait_recv()
                    merge = lambda at: (buf[c, b, at].astype(f32) + part[b, at].astype(f32)).astype(bf16)
                if T <= 4:
                    for o in range(lo, hi):
                        buf[c, b, o] = merge(o)
                else:

                    def one(o):
                        buf[c, b, o] = merge(o)

                    between(lo, hi, one)
                sum_copy(c, b, k, right).start()

    def hop_copy(c, b):
        cols = pl.ds(pl.multiple_of(b * DB, DB), DB)
        return pltpu.make_async_remote_copy(
            src_ref=xo.at[c, :, cols], dst_ref=gx.at[c, me, :, cols],
            send_sem=hop_send.at[c, b], recv_sem=hop_recv.at[c, b],
            device_id={"pp": s + 1}, device_id_type=MESH,
        )

    def out_copy(c, b):
        cols = pl.ds(pl.multiple_of(b * DB, DB), DB)
        return pltpu.make_async_copy(xo.at[c, :, cols], out_hbm.at[c, :, cols], out_sem.at[c, b])

    def finish(c, b):
        cols = pl.ds(pl.multiple_of(b * DB, DB), DB)
        acc[...] = part[b, me].astype(f32)
        if T > 1:

            @pl.when(me == T - 1)
            def _():
                sum_copy(c, b, T - 2, True).wait_recv()

            @pl.when(me == 0)
            def _():
                sum_copy(c, b, 1, False).wait_recv()

        @pl.when(has_left)
        def _():
            acc[...] += rr[c, b, me].astype(f32)

        @pl.when(has_right)
        def _():
            acc[...] += ll[c, b, me].astype(f32)

        xo[c, :, cols] = (gx[c, me, :, cols].astype(f32) + acc[...]).astype(bf16)
        out_copy(c, b).start()

        @pl.when(has_next)
        def _():
            hop_copy(c, b).start()

    last_hop = jnp.maximum(me, T - 1 - me)

    def rs_step(c, i):
        def at(lag, body):
            b = i - lag * HOP_TICKS

            @pl.when(jnp.logical_and(b >= 0, b < Nd))
            def _():
                body(b)

        at(me, lambda b: pass_on(c, b, True))
        at(T - 1 - me, lambda b: pass_on(c, b, False))
        at(last_hop, lambda b: finish(c, b))

    rs_steps = Nd + (T - 1) * HOP_TICKS
    pair = 2 if J % 2 == 0 else 1
    groups = J // pair
    spill = -(-(rs_steps - Nd) // groups)

    ticks = groups + Nd
    begin = jnp.where(s == 0, FIRST_BEGIN, LATER_BEGIN)

    def gathered(tick):
        done = jnp.clip((tick - begin + GATHER_TICKS) // GATHER_TICKS, 0, waves)
        return jnp.where(tick >= ticks - 1, waves, done)

    def communicate(c, tick):
        @pl.when(c + 1 < n)
        def _():
            lo = jnp.where(tick == 0, 0, gathered(tick - 1))
            between(lo, gathered(tick), lambda k: ag_step(c + 1, k))

    def member_side(sides, first):
        member = lax.broadcasted_iota(jnp.int32, sides.shape, 0) % members + first
        column = lax.broadcasted_iota(jnp.int32, sides.shape, 1)
        return jnp.sum(jnp.where(member == column, sides, 0.0), axis=1, keepdims=True)

    def add_side(product, side, right, cols):
        wide = product.reshape(T, ROWS, product.shape[-1])
        values = right[:, cols].astype(f32)
        member = lax.broadcasted_iota(jnp.int32, (ROWS, values.shape[1]), 0) % members
        rows_of = jnp.zeros((ROWS, values.shape[1]), f32)
        for m in range(members):
            rows_of = jnp.where(member == m, values[m : m + 1], rows_of)
        wide = wide + side[...].reshape(T, ROWS, 1) * rows_of[None]
        return wide.reshape(product.shape)

    NT = (((1,), (1,)), ((), ()))

    side_rows(gl, ul, lefts)
    side_rows(dl, None, downs)
    each(waves, lambda w: ag_step(0, w))

    @pl.when(has_next)
    def _():
        vectors.start()

    def chunk(c):
        each(T, lambda t: normalize(c, t))
        rows = lambda: xn[...]
        sides = coef_in * lax.dot_general(rows(), lefts[...], NT, preferred_element_type=f32)
        side_g[...] = member_side(sides, 0)
        side_u[...] = member_side(sides, members)

        def gu_half(j):
            if stream:
                q = c * stream + j - keep
                slot = jnp.where(j < keep, j, keep + (q + ring) % ring)
            else:
                q, slot = 0, j

            @pl.when(jnp.logical_or(c == 0, j >= keep))
            def _():
                for copy in gu_copies(j, slot):
                    copy.wait()

            cols = pl.ds(pl.multiple_of(j * HB, HB), HB)
            x = rows()
            gate = jnp.dot(x, wg[slot], preferred_element_type=f32)
            upper = jnp.dot(x, wu[slot], preferred_element_type=f32)
            gate = add_side(gate, side_g, gr, cols)
            upper = add_side(upper, side_u, ur, cols)
            hid[:, cols] = (gate / (1.0 + jnp.exp(-gate)) * upper).astype(bf16)
            return q, slot

        def refill(j, q, slot):
            if stream:
                ahead = q + ring

                @pl.when(jnp.logical_and(j >= keep, ahead < n * stream))
                def _():
                    start(gu_copies(keep + ahead % stream, slot))

        def gu(g):
            for u in range(pair):
                j = g * pair + u
                refill(j, *gu_half(j))

            @pl.when(c > 0)
            def _():
                between(Nd + g * spill, jnp.minimum(Nd + (g + 1) * spill, rs_steps), lambda i: rs_step(c - 1, i))

            communicate(c, g)

        each(groups, gu)

        @pl.when(jnp.logical_and(c == 0, has_next))
        def _():
            pl.semaphore_wait(ready, 1)

        side_d[...] = member_side(coef_hidden * lax.dot_general(hid[...], downs[...], NT, preferred_element_type=f32), 0)

        def down(b):
            q = c * Nd + b
            slot = q % dring
            cols = pl.ds(pl.multiple_of(b * DB, DB), DB)
            wd_copy(b, slot).wait()
            term = jnp.dot(hid[...], wd[slot], preferred_element_type=f32)
            part[b] = add_side(term, side_d, dr, cols).astype(bf16).reshape(T, ROWS, DB)

            @pl.when(q + dring < n * Nd)
            def _():
                wd_copy((b + dring) % Nd, slot).start()

            rs_step(c, b)
            communicate(c, groups + b)

        each(Nd, down)

    each(n, chunk)
    between(Nd, rs_steps, lambda i: rs_step(n - 1, i))

    @pl.when(has_next)
    def _():
        vectors.wait()

    def drain(c):
        def gather(g):
            for o in range(T):

                @pl.when(jnp.logical_and(has_right, o <= me))
                def _():
                    ag_copy(c, g, o, True).wait_send()

                @pl.when(jnp.logical_and(has_left, o >= me))
                def _():
                    ag_copy(c, g, o, False).wait_send()

        each(G, gather)

        def block(b):
            for right in (True, False):
                for k in senders(right):

                    @pl.when(me == k)
                    def _():
                        sum_copy(c, b, k, right).wait_send()

            out_copy(c, b).wait()

            @pl.when(has_next)
            def _():
                hop_copy(c, b).wait_send()

        each(Nd, block)

    each(n, drain)


class Exchange:

    def __init__(self, sources, targets, send, recv, own, p, count):
        self.copies = []
        for a, (source, target) in enumerate(zip(sources, targets)):
            self.copies.append(pltpu.make_async_copy(source, target.at[p], own.at[a]))
            for k in range(1, count):
                self.copies.append(
                    pltpu.make_async_remote_copy(
                        src_ref=source, dst_ref=target.at[p], send_sem=send.at[a, k - 1], recv_sem=recv.at[a, k - 1],
                        device_id={"pop": lax.rem(p + k, count)}, device_id_type=MESH,
                    )
                )

    def start(self):
        for copy in self.copies:
            copy.start()

    def wait(self):
        for copy in self.copies:
            copy.wait()


def gather_kernel(Pn, S, *refs):
    sources, targets, (send, recv, own) = refs[:7], refs[7:14], refs[14:]
    p = lax.axis_index("pop")

    @pl.when(lax.axis_index("pp") == S - 1)
    def _():
        barrier = pltpu.get_barrier_semaphore()
        for k in range(1, Pn):
            pl.semaphore_signal(barrier, inc=1, device_id={"pop": lax.rem(p + k, Pn)}, device_id_type=MESH)
        pl.semaphore_wait(barrier, Pn - 1)
        exchange = Exchange(sources, targets, send, recv, own, p, Pn)
        exchange.start()
        exchange.wait()


def updates_kernel(dims, *refs):
    Pn, members, share, D, F, block, last, aliased = dims
    gl, gr, ul, ur, dl, dr, fit = refs[:7]
    refs = refs[7 + aliased :]
    (out_gate, out_up, out_down), refs = refs[:3], refs[3:]
    if not aliased:
        refs[0][...] = jnp.zeros_like(refs[0])
        refs = refs[1:]
    left, right, weights, wide, tall, sem = refs
    population = members * Pn
    p, S = lax.axis_index("pop"), lax.axis_size("pp")
    here = lax.axis_index("pp")

    def spread(source, target, row, scaled):
        for k in range(Pn):
            at = slice(row + k * members, row + (k + 1) * members)
            values = source[k].astype(f32)
            target[at, 0 : values.shape[1]] = values * fit[k][:, :1] if scaled else values

    def product(source_left, source_right, out, stage, rows_total, row_first, col_first):
        columns = stage.shape[2]
        spread(source_left, left, 0, True)
        spread(source_right, right, 0, False)
        values = left[0:population]
        high = values.astype(bf16).astype(f32)
        left[0:population] = high
        left[population : 2 * population] = values - high
        right[population : 2 * population] = right[0:population]
        width = next(w for w in (512, 256, 128) if columns % w == 0)
        for j in range(0, columns, width):
            cols = pl.ds(pl.multiple_of(col_first + j, 128), width)
            weights[:, j : j + width] = right[:, cols].astype(bf16)
        count = rows_total // block

        def put(t, slot):
            rows = pl.ds(pl.multiple_of(t * block, block), block)
            return pltpu.make_async_copy(stage.at[slot], out.at[rows], sem.at[slot])

        def tile(t, z):
            slot = t % 2

            @pl.when(t >= 2)
            def _():
                put(t - 2, slot).wait()

            rows = pl.ds(pl.multiple_of(row_first + t * block, 128), block)
            lhs = left[:, rows].T.astype(bf16)
            for j in range(0, columns, width):
                got = jnp.dot(lhs, weights[:, j : j + width], preferred_element_type=f32)
                stage[slot, :, j : j + width] = got.astype(bf16)
            put(t, slot).start()
            return z

        lax.fori_loop(0, count, tile, 0)
        for t in range(max(0, count - 2), count):
            put(t, t % 2).wait()

    @pl.when(here == S - 1 if last else here < S - 1)
    def _():
        product(gl, gr, out_gate, wide, share, p * share, 0)
        product(ul, ur, out_up, wide, share, p * share, 0)
        product(dl, dr, out_down, tall, F, 0, p * share)


def gather(vectors):
    Pn, S = lax.axis_size("pop"), lax.axis_size("pp")
    dma = pltpu.SemaphoreType.DMA
    vmem, hbm = pl.BlockSpec(memory_space=pltpu.VMEM), pl.BlockSpec(memory_space=pl.ANY)
    return pl.pallas_call(
        functools.partial(gather_kernel, Pn, S),
        out_shape=tuple(jax.ShapeDtypeStruct((Pn,) + v.shape, v.dtype) for v in vectors),
        in_specs=[vmem] * 7,
        out_specs=(hbm,) * 7,
        scratch_shapes=[dma((7, max(1, Pn - 1))), dma((7, max(1, Pn - 1))), dma((7,))],
        compiler_params=pltpu.CompilerParams(collective_id=1, has_side_effects=True),
    )(*vectors)


def updates(everyone, before, after):
    Pn, members, D = everyone[0].shape
    F = everyone[1].shape[2]
    share = D // Pn
    block = next(w for w in (256, 128) if share % w == 0 and F % w == 0)
    last = before is None
    extra = [] if last else list(before) + [after]
    vmem, hbm = pl.BlockSpec(memory_space=pltpu.VMEM), pl.BlockSpec(memory_space=pl.ANY)
    shapes = [(share, F), (share, F), (F, share)]
    rows = 2 * members * Pn
    return pl.pallas_call(
        functools.partial(updates_kernel, (Pn, members, share, D, F, block, last, len(extra))),
        out_shape=tuple(jax.ShapeDtypeStruct(v, bf16) for v in shapes)
        + ((jax.ShapeDtypeStruct((8, 128), f32),) if last else ()),
        in_specs=[vmem] * 7 + [hbm] * len(extra),
        out_specs=(hbm,) * 3 + ((vmem,) if last else ()),
        input_output_aliases={} if last else {7: 0, 8: 1, 9: 2},
        scratch_shapes=[
            pltpu.VMEM((rows, max(D, F)), f32),
            pltpu.VMEM((rows, max(D, F)), f32),
            pltpu.VMEM((rows, max(F, share)), bf16),
            pltpu.VMEM((2, block, F), bf16),
            pltpu.VMEM((2, block, share), bf16),
            pltpu.SemaphoreType.DMA((2,)),
        ],
        compiler_params=pltpu.CompilerParams(has_side_effects=True),
    )(*everyone, *extra)


def relay(x, w_gate, w_up, w_down, gain, vectors, token):
    n, _, D = x.shape
    F = w_gate.shape[1]
    members = vectors[0].shape[0]
    T, S, Pn = (lax.axis_size(a) for a in ("tp", "pp", "pop"))
    HB, DB = widths(D, F)
    J, Nd, M = F // HB, D // DB, T * ROWS
    G = Nd // 2 if Nd % 2 == 0 else Nd
    dring = min(3, Nd)
    side = -(-2 * members // 16) * 16
    fixed = 2 * (n * ROWS * D + M * D + n * M * D + M * F + M * D + 2 * n * M * D + dring * F * DB + 4 * side * max(D, F)) + RESERVE
    slots = min(J, (VMEM_BYTES - fixed) // (4 * D * HB))
    ring = 0 if slots == J else min(3, slots)
    keep = slots - ring
    dims = (n, T, S, Pn, members, D, F, HB, DB, keep, ring, dring)
    vmem, hbm = pl.BlockSpec(memory_space=pltpu.VMEM), pl.BlockSpec(memory_space=pl.ANY)
    dma = pltpu.SemaphoreType.DMA
    return pl.pallas_call(
        functools.partial(relay_kernel, dims),
        out_shape=(jax.ShapeDtypeStruct((n, ROWS, D), bf16),)
        + tuple(jax.ShapeDtypeStruct((Pn,) + v.shape, v.dtype) for v in vectors),
        in_specs=[hbm] * 4 + [vmem] * 9,
        out_specs=(hbm,) * 8,
        scratch_shapes=[
            pltpu.VMEM((n, T, ROWS, D), bf16),
            pltpu.VMEM((M, D), bf16),
            pltpu.VMEM((M, F), bf16),
            pltpu.VMEM((Nd, T, ROWS, DB), bf16),
            pltpu.VMEM((n, Nd, T, ROWS, DB), bf16),
            pltpu.VMEM((n, Nd, T, ROWS, DB), bf16),
            pltpu.VMEM((n, ROWS, D), bf16),
            pltpu.VMEM((ROWS, DB), f32),
            pltpu.VMEM((M, 1), f32),
            pltpu.VMEM((M, 1), f32),
            pltpu.VMEM((M, 1), f32),
            pltpu.VMEM((slots, D, HB), bf16),
            pltpu.VMEM((slots, D, HB), bf16),
            pltpu.VMEM((dring, F, DB), bf16),
            pltpu.VMEM((side, max(D, F)), f32),
            pltpu.VMEM((side, D), bf16),
            pltpu.VMEM((side, F), bf16),
            dma((slots, 2)),
            dma((dring,)),
            dma((n, Nd)),
            dma((n, Nd)),
            dma((n, Nd)),
            dma((n, G, T)),
            dma((n, G, T)),
            dma((n, G, T)),
            dma((n, Nd)),
            dma((n, Nd)),
            dma((n, Nd)),
            dma((n, Nd)),
            dma((7, max(1, Pn - 1))),
            dma((7, max(1, Pn - 1))),
            dma((7,)),
            pltpu.SemaphoreType.REGULAR,
        ],
        compiler_params=pltpu.CompilerParams(collective_id=0, has_side_effects=True, vmem_limit_bytes=67_000_000),
    )(x, w_gate, w_up, w_down, gain, *vectors, token)


def per_device(
    hidden_in, norm_gain, w_gate, w_up, w_down,
    gate_left, gate_right, up_left, up_right, down_left, down_right, ranks,
):
    tokens, members, D = hidden_in.shape
    population = members * lax.axis_size("pop")
    fitness = (2.0 * ranks.astype(f32) / (population - 1) - 1.0) / math.sqrt(population)
    vectors = [gate_left[0], gate_right[0], up_left[0], up_right[0], down_left[0], down_right[0]]
    vectors.append(jnp.broadcast_to(fitness[:, None], (members, 128)))
    *last, token = updates(gather(vectors), None, None)
    x = hidden_in.reshape(tokens * members // ROWS, ROWS, D)
    out, *everyone = relay(x, w_gate[0], w_up[0], w_down[0], norm_gain, vectors, token)
    update_gate, update_up, update_down = updates(everyone, last, out)
    return (out.reshape(1, tokens, members, D), update_gate[None], update_up[None], update_down[None])


def solution(mesh):
    placed = (
        P("tp", "pop", None),
        P("pp", None),
        P("pp", None, "tp"),
        P("pp", None, "tp"),
        P("pp", "tp", None),
        P("pp", "pop", None),
        P("pp", "pop", "tp"),
        P("pp", "pop", None),
        P("pp", "pop", "tp"),
        P("pp", "pop", "tp"),
        P("pp", "pop", None),
        P("pop"),
    )
    return jax.shard_map(
        per_device,
        mesh=mesh,
        in_specs=placed,
        out_specs=(
            P("pp", "tp", "pop", None),
            P("pp", "pop", "tp"),
            P("pp", "pop", "tp"),
            P("pp", "tp", "pop"),
        ),
        check_vma=False,
    )
```

time: 260 us -> 218 us (0.84); the launches traced: 256 us -> 217 us
  matrix products: 13.6 us -> 0 us
  local copies, waits for them, and re-layouts: 18 us -> 4.68 us
  Pallas kernels: 221 us -> 211 us
    pallas_call x1, Pallas kernels: 221 us -> 184 us  [relay(): pl.pallas_call(functools.partial(relay_kernel, dims), out_shape=(jax.Shap...]
    pallas_call x0 -> x3, Pallas kernels: none -> 26.4 us  [the longest x2 18.4 us: updates(): pl.pallas_call(functools.partial(updates_kernel, (Pn, members, share, D,...]
    dot_general x3 -> x0, matrix products: 13.6 us -> none  [low_rank(): jnp.einsum('pi,pj->ij', both, jnp.concatenate([right, right]), preferred_...]
    another operation x12 -> x0, local copies, waits for them, and re-layouts: 9.23 us -> none  [the longest x6 4.85 us: expand(): return jnp.tile(vectors, (ROWS // members, 1))]
where the time goes in v2:
time: 218 us; the launch traced here: 217 us
  Pallas kernels  211 us (97%)
  local copies, waits for them, and re-layouts  4.68 us (2%)
    pallas_call x1, Pallas kernels, relay(): pl.pallas_call(functools.partial(relay_kernel, dims), out_shape=(jax.Shap...  184 us
    pallas_call x2, Pallas kernels, updates(): pl.pallas_call(functools.partial(updates_kernel, (Pn, members, share, D,...  18.4 us
    pallas_call x1, Pallas kernels, gather(): pl.pallas_call(functools.partial(gather_kernel, Pn, S), out_shape=tuple((...  8.05 us

profile of v2, /device:TPU:6, one launch (start us, length us, event | category | flops | bytes accessed | tf_op | source)
XLA Modules:
  0.0 216.8 jit_solution(6019049050903548134)
XLA Ops:
  0.6 0.7 add_multiply_fusion
  1.3 0.6 broadcast_in_dim.15.refs_6_.fit
  1.9 8.0 %shard_map.147 = (bf16[4,2,4096]{2,1,0:T(2,128)(2,1)}, bf16[4,2,3072]{2,1,0:T(2,128)(2,1)}, bf16[4,2,4096]{2,1,0:T(2,128)(2,1)}, bf16[4,2,3072]{2,1,0:T(2,128)(2...) custom-call(bf16[2,4096]{1,0:T(2,128)(2,1)} %bitcast.18, ...), custom_call_target="tpu_custom_call" | custom-call | tf_op jit(solution)/shard_map/pallas_call | solution.py:516
  10.0 2.2 %reshape.15.x_hbm = bf16[4,32,4096]{2,1,0:T(8,128)(2,1)} reshape(bf16[64,2,4096]{2,1,0:T(2,128)(2,1)} %param.12) | data formatting | bytes 2097152 | tf_op jit(solution)/shard_map/reshape | solution.py:627
  12.2 17.3 %shard_map.148 = (bf16[1024,3072]{1,0:T(8,128)(2,1)}, bf16[1024,3072]{1,0:T(8,128)(2,1)}, bf16[3072,1024]{1,0:T(8,128)(2,1)}, f32[8,128]{1,0:T(8,128)}) custom-call(bf16[4,2,4096]{2,1,0:T(2,128)(2,1)} %get-tuple-element.26.refs_0_, bf16[4,2,3072]{2,1,0:T(2,128)(2,1)} %get-tuple-element.27.refs_1_, bf16[4,2,4096]{2,1,0:T(2,128)(2,1)} %get-tuple-element.28.refs_2_, ...), custom_call_target="tpu_custom_call" | custom-call | tf_op jit(solution)/shard_map/pallas_call | solution.py:536
  29.6 184.4 %shard_map.149 = (bf16[4,32,4096]{2,1,0:T(8,128)(2,1)}, bf16[4,2,4096]{2,1,0:T(2,128)(2,1)}, bf16[4,2,3072]{2,1,0:T(2,128)(2,1)}, bf16[4,2,4096]{2,1,0:T(2,128)(...) custom-call(bf16[4,32,4096]{2,1,0:T(8,128)(2,1)} %reshape.15.x_hbm, ...), custom_call_target="tpu_custom_call" | custom-call | tf_op jit(solution)/shard_map/pallas_call | solution.py:572
  213.9 0.0 copy-start
  213.9 1.1 shard_map.150
  215.0 0.3 copy-done
  215.3 1.5 reshape.16
Async XLA Ops:
  213.9 1.4 copy-start

commit v3 on v2

--- a/solution.py
+++ b/solution.py
@@ -16,9 +16,10 @@
 
 ROWS = 32
 HOP_TICKS = 4
-GATHER_TICKS = 2
-FIRST_BEGIN = 1
-LATER_BEGIN = 3
+GATHER_TICKS = 3
+FIRST_BEGIN = 0
+FIRST_PAUSE = 7
+LATER_BEGIN = 1
 VMEM_BYTES = 66_000_000
 RESERVE = 1_500_000
 
@@ -142,14 +143,28 @@
             ag_copy(c, g, me + k, False).wait_recv()
             ag_send(c, g, me + k, has_left, False)
 
-    waves = G + T - 1
-
-    def ag_step(c, w):
-        @pl.when(w < G)
-        def _():
-            ag_own(c, w)
-
-        between(jnp.maximum(1, w - G + 1), jnp.minimum(w, T - 1) + 1, lambda k: ag_pass(c, w - k, k))
+    steps = jnp.where(s == 0, G * T, G + T - 1)
+
+    def ag_step(c, i):
+        @pl.when(s == 0)
+        def _():
+            k, g = i // G, i % G
+
+            @pl.when(k == 0)
+            def _():
+                ag_own(c, g)
+
+            @pl.when(k > 0)
+            def _():
+                ag_pass(c, g, k)
+
+        @pl.when(s > 0)
+        def _():
+            @pl.when(i < G)
+            def _():
+                ag_own(c, i)
+
+            between(jnp.maximum(1, i - G + 1), jnp.minimum(i, T - 1) + 1, lambda k: ag_pass(c, i - k, k))
 
     def normalize(c, t):
         total = jnp.zeros((ROWS, 1), f32)
@@ -253,7 +268,7 @@
         at(last_hop, lambda b: finish(c, b))
 
     rs_steps = Nd + (T - 1) * HOP_TICKS
-    pair = 2 if J % 2 == 0 else 1
+    pair = 1
     groups = J // pair
     spill = -(-(rs_steps - Nd) // groups)
 
@@ -261,8 +276,10 @@
     begin = jnp.where(s == 0, FIRST_BEGIN, LATER_BEGIN)
 
     def gathered(tick):
-        done = jnp.clip((tick - begin + GATHER_TICKS) // GATHER_TICKS, 0, waves)
-        return jnp.where(tick >= ticks - 1, waves, done)
+        first = jnp.where(tick < begin, 0, G + (jnp.maximum(tick - begin - FIRST_PAUSE, 0) * G * (T - 1)) // max(1, ticks - FIRST_PAUSE - 2))
+        later = (tick - begin + GATHER_TICKS) // GATHER_TICKS
+        done = jnp.clip(jnp.where(s == 0, first, later), 0, steps)
+        return jnp.where(tick >= ticks - 1, steps, done)
 
     def communicate(c, tick):
         @pl.when(c + 1 < n)
@@ -289,7 +306,7 @@
 
     side_rows(gl, ul, lefts)
     side_rows(dl, None, downs)
-    each(waves, lambda w: ag_step(0, w))
+    each(steps, lambda i: ag_step(0, i))
 
     @pl.when(has_next)
     def _():

time: 218 us -> 212 us (0.972)
  Pallas kernels: 211 us -> 205 us
    pallas_call x1, Pallas kernels: 184 us -> 179 us  [relay(): pl.pallas_call(functools.partial(relay_kernel, dims), out_shape=(jax.Shap...]
where the time goes in v3:
time: 212 us; the launch traced here: 211 us
  Pallas kernels  205 us (97%)
  local copies, waits for them, and re-layouts  4.68 us (2%)
    pallas_call x1, Pallas kernels, relay(): pl.pallas_call(functools.partial(relay_kernel, dims), out_shape=(jax.Shap...  179 us
    pallas_call x2, Pallas kernels, updates(): pl.pallas_call(functools.partial(updates_kernel, (Pn, members, share, D,...  18.4 us
    pallas_call x1, Pallas kernels, gather(): pl.pallas_call(functools.partial(gather_kernel, Pn, S), out_shape=tuple((...  8.05 us

profile of v3, /device:TPU:6, one launch (start us, length us, event | category | flops | bytes accessed | tf_op | source)
XLA Modules:
  0.0 211.2 jit_solution(10867412395247069327)
XLA Ops:
  0.6 0.7 add_multiply_fusion
  1.3 0.6 broadcast_in_dim.15.refs_6_.fit
  1.9 8.0 %shard_map.147 = (bf16[4,2,4096]{2,1,0:T(2,128)(2,1)}, bf16[4,2,3072]{2,1,0:T(2,128)(2,1)}, bf16[4,2,4096]{2,1,0:T(2,128)(2,1)}, bf16[4,2,3072]{2,1,0:T(2,128)(2...) custom-call(bf16[2,4096]{1,0:T(2,128)(2,1)} %bitcast.18, ...), custom_call_target="tpu_custom_call" | custom-call | tf_op jit(solution)/shard_map/pallas_call | solution.py:533
  10.0 2.2 %reshape.15.x_hbm = bf16[4,32,4096]{2,1,0:T(8,128)(2,1)} reshape(bf16[64,2,4096]{2,1,0:T(2,128)(2,1)} %param.12) | data formatting | bytes 2097152 | tf_op jit(solution)/shard_map/reshape | solution.py:644
  12.2 17.3 %shard_map.148 = (bf16[1024,3072]{1,0:T(8,128)(2,1)}, bf16[1024,3072]{1,0:T(8,128)(2,1)}, bf16[3072,1024]{1,0:T(8,128)(2,1)}, f32[8,128]{1,0:T(8,128)}) custom-call(bf16[4,2,4096]{2,1,0:T(2,128)(2,1)} %get-tuple-element.26.refs_0_, bf16[4,2,3072]{2,1,0:T(2,128)(2,1)} %get-tuple-element.27.refs_1_, bf16[4,2,4096]{2,1,0:T(2,128)(2,1)} %get-tuple-element.28.refs_2_, ...), custom_call_target="tpu_custom_call" | custom-call | tf_op jit(solution)/shard_map/pallas_call | solution.py:553
  29.6 178.8 %shard_map.149 = (bf16[4,32,4096]{2,1,0:T(8,128)(2,1)}, bf16[4,2,4096]{2,1,0:T(2,128)(2,1)}, bf16[4,2,3072]{2,1,0:T(2,128)(2,1)}, bf16[4,2,4096]{2,1,0:T(2,128)(...) custom-call(bf16[4,32,4096]{2,1,0:T(8,128)(2,1)} %reshape.15.x_hbm, ...), custom_call_target="tpu_custom_call" | custom-call | tf_op jit(solution)/shard_map/pallas_call | solution.py:589
  208.4 0.0 copy-start
  208.4 1.1 shard_map.150
  209.4 0.3 copy-done
  209.8 1.5 reshape.16
Async XLA Ops:
  208.4 1.4 copy-start
